TPU v7x, 32 devices: a whole 2x2x4 slice. The times are simulated.
32 devices in a mesh: dp: 8 (over y, x, core), mp: 4 (over z).
Axes of the slice: x: 2, y: 2, z: 4, core: 2. Of those that a mesh axis runs over, the one named last changes fastest.
Arguments:
- mel_audio: bfloat16 [32, 80, 2048], P('dp'), may hold values from -6 to 6
- start_noise: bfloat16 [32, 80, 1024], P('dp'), may hold values from -6 to 6
- span_start: int32 [32], replicated, may hold values from 0 to 2047, as said below
- span_length: int32 [32], replicated, may hold values from 1 to 1024, as said below
- block_route: int32 [128], replicated, may hold values from -1 to 47, as said below
- w_input: bfloat16 [160, 1024], replicated, may hold values from -0.5 to 0.5
- attn_gain: float32 [1024], replicated, may hold values from 0.1 to 1.9
- w_qkv: bfloat16 [1024, 3, 1024], P(None, None, 'mp'), may hold values from -4 to 4, as said below
- w_out: bfloat16 [1024, 1024], P('mp'), may hold values from -0.1875 to 0.1875
- final_gain: float32 [1024], replicated, may hold values from 0.1 to 1.9
- w_mel: bfloat16 [80, 1024], replicated, may hold values from -0.1875 to 0.1875
Outputs:
- infilled: float32 [32, 80, 1024], P('dp')
- worker_velocity: float32 [48, 80, 256], P('dp')
Inputs may be any that keep to these rules, and one draw needn't show every extreme that they name: Each span lies inside its utterance: span_start[u] + span_length[u] <= 2048. `span_length`: the spans cover 48 blocks of 256 frames in all (the last block of a span may be partly filled). `block_route`: live block slots name worker slots w * 6 + j of worker w, each worker slot exactly once; empty slots hold -1. No worker receives more than 2 blocks from the utterances of one dp index (utterances u with the same u // 4), and some worker receives exactly 2 from one. `w_qkv`: Query, key and value projections in that order along the middle dimension.
All inputs are finite; a program needn't handle non-finite values.
Results may differ from a plain program's by a relative error of at most 0.025.
Values may be sent and summed in bfloat16 or wider, within the bound.
A program may use at most 128 MiB of HBM per device.

v0:
```python
import math

import jax
import jax.numpy as jnp
from jax import lax
from jax.experimental import pallas as pl
from jax.experimental.pallas import tpu as pltpu
from jax.sharding import PartitionSpec as P

MEL = 80
HEAD_DIM = 64
BLOCK = 256
CTX = 128
BLK_UTT = 4
UTT_DEV = 4
WORK_DEV = 6
EULER = 2
FRAMES = 2048
WIN = 512
SPAN_MAX = 1024
SLOT_DEV = 16


flow_steps = 32.0
norm_eps = 1e-05


def time_embed(t_value, feature_width):
    half_width = feature_width // 2
    freqs = jnp.exp(-math.log(10000.0) * jnp.arange(half_width, dtype=jnp.float32) / half_width)
    angles = 1000.0 * t_value * freqs
    return jnp.concatenate([jnp.sin(angles), jnp.cos(angles)])


def layer_norm(hidden, norm_gain):
    mean_value = jnp.mean(hidden, axis=-1, keepdims=True)
    centred = hidden - mean_value
    variance = jnp.mean(centred * centred, axis=-1, keepdims=True)
    return centred * lax.rsqrt(variance + norm_eps) * norm_gain


def owner_windows(mel_part, noise_part, first_frames, lengths):
    channels = mel_part.shape[1]
    reach = SPAN_MAX + 2 * CTX
    padded = jnp.pad(mel_part, ((0, 0), (0, 0), (CTX, SPAN_MAX + CTX)))
    regions = jnp.stack(
        [lax.dynamic_slice_in_dim(padded[u], first_frames[u], reach, 1) for u in range(UTT_DEV)]
    )
    offsets = jnp.arange(reach, dtype=jnp.int32)[None, :] - CTX
    in_span = (offsets >= 0) & (offsets < lengths[:, None])
    regions = jnp.where(in_span[:, None, :], jnp.zeros((), jnp.bfloat16), regions)
    live_mask = jnp.arange(SPAN_MAX, dtype=jnp.int32)[None, :] < lengths[:, None]
    current = jnp.where(live_mask[:, None, :], noise_part, jnp.zeros((), jnp.bfloat16))
    blocks = [
        jnp.concatenate(
            [
                regions[:, :, BLOCK * k : BLOCK * k + WIN],
                current[:, :, BLOCK * k : BLOCK * (k + 1)],
            ],
            axis=2,
        )
        for k in range(BLK_UTT)
    ]
    return jnp.stack(blocks, axis=1).reshape(SLOT_DEV, channels, WIN + BLOCK)


def owner_targets(block_route, dp_count, capacity):
    owner_index = lax.axis_index("dp")
    destination = lax.dynamic_slice_in_dim(block_route, owner_index * SLOT_DEV, SLOT_DEV, 0)
    live = destination >= 0
    worker = jnp.where(live, destination // WORK_DEV, -1)
    earlier = (
        (worker[:, None] == worker[None, :])
        & (destination[None, :] < destination[:, None])
        & live[None, :]
    )
    rank = jnp.sum(earlier.astype(jnp.int32), axis=1)
    position = worker * capacity + rank
    rows = jnp.arange(dp_count * capacity, dtype=jnp.int32)
    return (rows[:, None] == position[None, :]) & live[None, :]


def worker_plan(block_route, span_start, span_length, dp_count, capacity):
    worker_index = lax.axis_index("dp")
    slot_ids = worker_index * WORK_DEV + jnp.arange(WORK_DEV, dtype=jnp.int32)
    every_slot = jnp.arange(block_route.shape[0], dtype=jnp.int32)
    matches = block_route[None, :] == slot_ids[:, None]
    block_index = jnp.sum(jnp.where(matches, every_slot[None, :], 0), axis=1)
    owner = block_index // SLOT_DEV
    utterance = block_index // BLK_UTT
    block_order = block_index % BLK_UTT
    utter_ids = jnp.arange(span_start.shape[0], dtype=jnp.int32)
    pick_utter = utterance[:, None] == utter_ids[None, :]
    first_frame = jnp.sum(jnp.where(pick_utter, span_start[None, :], 0), axis=1)
    length = jnp.sum(jnp.where(pick_utter, span_length[None, :], 0), axis=1)
    window_begin = first_frame + BLOCK * block_order
    own_count = jnp.minimum(BLOCK, length - BLOCK * block_order)
    local_ids = jnp.arange(WORK_DEV, dtype=jnp.int32)
    earlier = (owner[:, None] == owner[None, :]) & (local_ids[None, :] < local_ids[:, None])
    rank = jnp.sum(earlier.astype(jnp.int32), axis=1)
    position = owner * capacity + rank
    pick_owner = position[:, None] == jnp.arange(dp_count * capacity, dtype=jnp.int32)[None, :]
    return (pick_owner, window_begin, own_count)


def attention_kernel(own_ref, rows_ref, usable_ref, weight_ref, out_ref):
    depth, columns = rows_ref.shape[1], weight_ref.shape[4]

    def project(rows, i):
        weight = weight_ref[:, 0, i].reshape(depth, columns)
        return jnp.dot(rows[...], weight, preferred_element_type=jnp.float32).astype(
            jnp.bfloat16
        )

    queries = project(own_ref, 0)
    key_rows = project(rows_ref, 1)
    value_rows = project(rows_ref, 2)
    width = queries.shape[1]
    head_of_lane = lax.broadcasted_iota(jnp.int32, (1, width), 1) // HEAD_DIM
    for block, (begin, end) in enumerate(((0, BLOCK), (BLOCK, own_ref.shape[0]))):
        block_queries = queries[begin:end]
        block_keys = key_rows[block * WIN : (block + 1) * WIN]
        block_values = value_rows[block * WIN : (block + 1) * WIN]
        usable = usable_ref[block : block + 1, :] > 0
        collected = jnp.zeros((end - begin, width), jnp.float32)
        for head in range(width // HEAD_DIM):
            mine = head_of_lane == head
            head_queries = jnp.where(mine, block_queries, jnp.zeros((), jnp.bfloat16))
            scores = lax.dot_general(
                head_queries,
                block_keys,
                (((1,), (1,)), ((), ())),
                preferred_element_type=jnp.float32,
            )
            scores = jnp.where(usable, scores * (1.0 / math.sqrt(HEAD_DIM)), -1e30)
            weights = jnp.exp(scores - jnp.max(scores, axis=1, keepdims=True))
            norm = jnp.sum(weights, axis=1, keepdims=True)
            product = jnp.dot(
                weights.astype(jnp.bfloat16), block_values, preferred_element_type=jnp.float32
            )
            collected = jnp.where(mine, product * (1.0 / norm), collected)
        out_ref[begin:end, :] = collected.astype(jnp.bfloat16)


def attention(own, rows, usable, w_parts):
    parts, groups, kinds, part_rows, columns = w_parts.shape
    count, depth = own.shape
    return pl.pallas_call(
        attention_kernel,
        grid=(groups,),
        out_shape=jax.ShapeDtypeStruct((count, groups * columns), jnp.bfloat16),
        in_specs=[
            pl.BlockSpec((count, depth), lambda g: (0, 0)),
            pl.BlockSpec(rows.shape, lambda g: (0, 0)),
            pl.BlockSpec(usable.shape, lambda g: (0, 0)),
            pl.BlockSpec(
                (parts, 1, kinds, part_rows, columns), lambda g: (0, g, 0, 0, 0)
            ),
        ],
        out_specs=pl.BlockSpec((count, columns), lambda g: (0, g)),
        cost_estimate=pl.CostEstimate(
            flops=2 * groups * columns * depth * (count + 2 * rows.shape[0]) * 2,
            bytes_accessed=3 * groups * depth * columns * 2,
            transcendentals=count * WIN * groups * columns // HEAD_DIM,
        ),
        compiler_params=pltpu.CompilerParams(vmem_limit_bytes=40 * 1024 * 1024),
    )(own, rows, usable, w_parts)


def block_velocity(window, usable, first_row, row_count, t_value, weights):
    w_input, attn_gain, w_parts, w_out, final_gain, w_mel = weights
    hidden = jnp.einsum("scf,cd->sfd", window, w_input, preferred_element_type=jnp.float32)
    hidden = hidden + time_embed(t_value, w_input.shape[1])[None, None, :]
    normed = layer_norm(hidden, attn_gain).astype(jnp.bfloat16)

    def own_rows(rows):
        second = lax.dynamic_slice_in_dim(rows[1], CTX + first_row, row_count, 0)
        return jnp.concatenate([rows[0, CTX : CTX + BLOCK], second], axis=0)

    head_outputs = attention(
        own_rows(normed), normed.reshape(2 * WIN, normed.shape[2]), usable, w_parts
    )
    attended = jnp.dot(head_outputs, w_out, preferred_element_type=jnp.float32)
    final = layer_norm(own_rows(hidden) + attended, final_gain).astype(jnp.bfloat16)
    return jnp.einsum("md,qd->mq", w_mel, final, preferred_element_type=jnp.float32)


def gather_weights(w_qkv, w_out):
    dp_count = lax.axis_size("dp")
    mp_count = lax.axis_size("mp")
    dp_index = lax.axis_index("dp")
    depth, columns = w_qkv.shape[0], w_qkv.shape[2]
    rows = depth // dp_count
    part = lax.dynamic_slice_in_dim(w_qkv, dp_index * rows, rows, 0).transpose(1, 0, 2)
    w_parts = lax.all_gather(part, ("dp", "mp"), axis=0, tiled=False)
    w_parts = w_parts.reshape(dp_count, mp_count, 3, rows, columns)
    out_rows = w_out.shape[0] // dp_count
    out_part = lax.dynamic_slice_in_dim(w_out, dp_index * out_rows, out_rows, 0)
    out_parts = lax.all_gather(out_part, ("dp", "mp"), axis=0, tiled=False)
    out_parts = out_parts.reshape(dp_count, mp_count, out_rows, w_out.shape[1])
    return w_parts, out_parts.transpose(1, 0, 2, 3).reshape(-1, w_out.shape[1])


def to_span(slot_values):
    return (
        slot_values.reshape(UTT_DEV, BLK_UTT, MEL, BLOCK)
        .transpose(0, 2, 1, 3)
        .reshape(UTT_DEV, MEL, SPAN_MAX)
    )


def shards(
    mel_audio,
    start_noise,
    span_start,
    span_length,
    block_route,
    w_input,
    attn_gain,
    w_qkv,
    w_out,
    final_gain,
    w_mel,
):
    dp_count = lax.axis_size("dp")
    capacity = (SLOT_DEV + dp_count - 1) // dp_count
    owner_index = lax.axis_index("dp")
    first_frames = lax.dynamic_slice_in_dim(span_start, owner_index * UTT_DEV, UTT_DEV, 0)
    lengths = lax.dynamic_slice_in_dim(span_length, owner_index * UTT_DEV, UTT_DEV, 0)
    targets = owner_targets(block_route, dp_count, capacity)
    target_rows = targets.astype(jnp.bfloat16)
    pick_owner, window_begin, own_count = worker_plan(
        block_route, span_start, span_length, dp_count, capacity
    )
    w_parts, w_out_all = gather_weights(w_qkv, w_out)
    weights = (w_input, attn_gain, w_parts, w_out_all, final_gain, w_mel)
    mp_count = lax.axis_size("mp")
    mp_index = lax.axis_index("mp")
    group = 2 * WORK_DEV // mp_count
    channels = MEL // mp_count
    mel_part = lax.dynamic_slice_in_dim(mel_audio, mp_index * channels, channels, 1)
    noise_part = lax.dynamic_slice_in_dim(start_noise, mp_index * channels, channels, 1)
    windows = owner_windows(mel_part, noise_part, first_frames, lengths)
    outgoing = jnp.einsum(
        "ws,scf->wcf", target_rows, windows, preferred_element_type=jnp.float32
    ).astype(jnp.bfloat16)
    received = lax.all_to_all(outgoing, "dp", split_axis=0, concat_axis=0, tiled=True)
    pairs = []
    for m in range(mp_count):
        pairs += [group * (m // 2) + (group - 1) * (m % 2), group * (m // 2) + 1]
    pick_pairs = jnp.concatenate([pick_owner[j : j + 1] for j in pairs], axis=0)
    spread = jnp.einsum(
        "so,ocf->scf",
        pick_pairs.astype(jnp.bfloat16),
        received,
        preferred_element_type=jnp.float32,
    ).astype(jnp.bfloat16)
    mine = lax.all_to_all(spread, "mp", split_axis=0, concat_axis=0, tiled=True)
    mine = mine.reshape(mp_count, 2, channels, WIN + BLOCK).transpose(1, 0, 2, 3)
    mine = mine.reshape(2, MEL, WIN + BLOCK)
    pair_begin = lax.dynamic_slice_in_dim(
        jnp.stack([window_begin[j] for j in pairs]), 2 * mp_index, 2, 0
    )
    pair_count = lax.dynamic_slice_in_dim(
        jnp.stack([own_count[j] for j in pairs]), 2 * mp_index, 2, 0
    )
    position = pair_begin[:, None] - CTX + jnp.arange(WIN, dtype=jnp.int32)[None, :]
    usable = ((position >= 0) & (position < FRAMES)).astype(jnp.int32)
    columns = jnp.arange(BLOCK, dtype=jnp.int32)
    live_mask = columns[None, :] < pair_count[:, None]
    half = BLOCK // 2
    first_row = (mp_index % 2) * half
    context = mine[:, :, :WIN]
    block_state = mine[:, :, WIN:].astype(jnp.float32)
    half_total = jnp.zeros((MEL, BLOCK + half), jnp.float32)
    for euler_step in range(EULER):
        state_rows = jnp.where(live_mask[:, None, :], block_state, 0.0).astype(jnp.bfloat16)
        state_window = jnp.pad(state_rows, ((0, 0), (0, 0), (CTX, CTX)))
        window = jnp.concatenate([context, state_window], axis=1)
        last = euler_step == EULER - 1
        row_begin, row_count = (first_row, half) if last else (0, BLOCK)
        result = block_velocity(
            window, usable, row_begin, row_count, euler_step / flow_steps, weights
        )
        if last:
            own_live = jnp.concatenate(
                [live_mask[0], lax.dynamic_slice_in_dim(live_mask[1], first_row, half, 0)]
            )
            velocity = jnp.where(own_live[None, :], result, 0.0)
            half_total = half_total + velocity
        else:
            both = jnp.stack([result[:, :BLOCK], result[:, BLOCK:]])
            both = jnp.where(live_mask[:, None, :], both, 0.0)
            block_state = block_state + both * (1.0 / flow_steps)
            own = lax.dynamic_slice_in_dim(both[1], first_row, half, 1)
            half_total = half_total + jnp.concatenate([both[0], own], axis=1)

    def whole_blocks(halves):
        blocks = []
        for pair in range(mp_count // 2):
            one, other = halves[2 * pair], halves[2 * pair + 1]
            middle = jnp.concatenate([one[:, BLOCK:], other[:, BLOCK:]], axis=1)
            blocks += [one[:, :BLOCK], middle, other[:, :BLOCK]]
        return jnp.stack(blocks)

    both = jnp.concatenate([half_total, velocity], axis=1).astype(jnp.bfloat16)
    both = lax.all_gather(both, "mp")
    finals = whole_blocks(both[:, :, : BLOCK + half])
    result = whole_blocks(both[:, :, BLOCK + half :]).astype(jnp.float32)
    returned = jnp.einsum(
        "so,smq->omq",
        pick_owner.astype(jnp.bfloat16),
        finals,
        preferred_element_type=jnp.float32,
    )
    arrived = lax.all_to_all(
        returned.astype(jnp.bfloat16), "dp", split_axis=0, concat_axis=0, tiled=True
    )
    slot_values = jnp.einsum(
        "ws,wmq->smq", target_rows, arrived, preferred_element_type=jnp.float32
    )
    infilled = to_span(slot_values)
    return (infilled, result)


def solution(mesh):
    return jax.shard_map(
        shards,
        mesh=mesh,
        in_specs=(
            P("dp", None, None),
            P("dp", None, None),
            P(),
            P(),
            P(),
            P(),
            P(),
            P(None, None, "mp"),
            P("mp", None),
            P(),
            P(),
        ),
        out_specs=(P("dp", None, None), P("dp", None, None)),
        check_vma=False,
    )
```

profile of v0, /device:TPU:0, one launch (start us, length us, event | category | flops | bytes accessed | tf_op | source)
XLA Modules:
  0.0 234.1 jit_solution(14046508511628249907)
XLA Ops:
  7.2 1.6 constant_dynamic-slice_fusion.1
  24.4 5.3 %all-to-all-start = ((bf16[16,20,768]{2,1,0:T(8,128)(2,1)}), bf16[16,20,768]{2,1,0:T(8,128)(2,1)S(1)}, u32[]{:S(2)}, u32[]{:S(2)}) async-start(bf16[16,20,768]{2,1,0:T(8,128)(2,1)} %copy.96), calls=%async_computation | async-start | bytes 1179648 | tf_op jit(solution)/shard_map/all_to_all | solution.py:247
  31.5 2.5 %pad_add_fusion.1 = (s32[8]{0:T(128)S(1)}, s32[8]{0:T(128)S(1)}) fusion(s32[1]{0:T(128)} %get-tuple-element.53, s32[3]{0:T(128)S(1)} %get-tuple-element.51, s32[1]{0:T(128)} %get-tuple-element.52, s32[3]{0:T(128)S(1)} %get-tuple-element.50, s32[1]{0:T(128)} %get-tuple-element.49, s32[3]{0:T(128)S(1)} %get-tuple-element.47, s32[1]{0:T(128)} %get-tuple-element.48, ...), kind=kLoop, calls=%fused_computation.170 | loop fusion | flops 48 | bytes 128 | tf_op jit(solution)/shard_map/stack | solution.py:265
  34.7 5.4 %all-to-all-done = bf16[16,20,768]{2,1,0:T(8,128)(2,1)S(1)} async-done(((bf16[16,20,768]{2,1,0:T(8,128)(2,1)}), bf16[16,20,768]{2,1,0:T(8,128)(2,1)S(1)}, u32[]{:S(2)}, u32[]{:S(2)}) %all-to-all-start) | async-done | bytes 491552 | tf_op jit(solution)/shard_map/all_to_all | solution.py:247
  41.1 4.8 %all-to-all-start.1 = ((bf16[8,20,768]{2,1,0:T(8,128)(2,1)}), bf16[8,20,768]{2,1,0:T(8,128)(2,1)S(1)}, u32[]{:S(2)}, u32[]{:S(2)}) async-start(bf16[8,20,768]{2,1,0:T(8,128)(2,1)} %copy.98), calls=%async_computation.1 | async-start | bytes 589824 | tf_op jit(solution)/shard_map/all_to_all | solution.py:258
  46.0 8.0 %all-to-all-done.1 = bf16[8,20,768]{2,1,0:T(8,128)(2,1)S(1)} async-done(((bf16[8,20,768]{2,1,0:T(8,128)(2,1)}), bf16[8,20,768]{2,1,0:T(8,128)(2,1)S(1)}, u32[]{:S(2)}, u32[]{:S(2)}) %all-to-all-start.1) | async-done | bytes 245792 | tf_op jit(solution)/shard_map/all_to_all | solution.py:258
  56.8 1.2 copy-done.1
  58.0 1.6 slice_bitcast_fusion.2
  59.7 13.1 %all-gather.7.cloned.1.call-done = bf16[1024,1024]{1,0:T(8,128)(2,1)} async-done(((bf16[32,1024]{1,0:T(8,128)(2,1)}), bf16[1024,1024]{1,0:T(8,128)(2,1)}) %all-gather.7.cloned.1.call-update) | async-done | bytes 2097168 | tf_op jit(solution)/shard_map/all_gather | solution.py:199
  72.8 3.2 %copy.102 = bf16[4,8,32,1024]{3,2,1,0:T(8,128)(2,1)} copy(bf16[4,8,32,1024]{3,2,0,1:T(8,128)(2,1)} %bitcast.157) | data formatting | bytes 4194304 | tf_op jit(solution)/shard_map/transpose | solution.py:201
  75.9 67.8 %all-gather.5.cloned.1.call-done = bf16[96,128,256]{2,1,0:T(8,128)(2,1)} async-done(((bf16[3,128,256]{2,1,0:T(8,128)(2,1)}), bf16[96,128,256]{2,1,0:T(8,128)(2,1)}) %all-gather.5.cloned.1.call-update) | async-done | bytes 6291472 | tf_op jit(solution)/shard_map/all_gather | solution.py:195
  143.8 1.6 copy-done.2
  145.4 2.8 %copy-done.3 = bf16[96,128,256]{2,1,0:T(8,128)(2,1)S(1)} copy-done((bf16[96,128,256]{2,1,0:T(8,128)(2,1)S(1)}, bf16[96,128,256]{2,1,0:T(8,128)(2,1)}, u32[]{:S(2)}) %copy-start.3) | copy-done | bytes 6291480
  148.2 14.4 %shard_map.122 = bf16[512,1024]{1,0:T(8,128)(2,1)S(1)} custom-call(bf16[512,1024]{1,0:T(8,128)(2,1)S(1)} %pad_maximum_fusion.own_ref, bf16[1024,1024]{1,0:T(8,128)(2,1)S(1)} %bitcast.149, s32[2,512]{1,0:T(2,128)S(1)} %and_convert_fusion.usable_ref, bf16[8,4,3,128,256]{4,3,2,1,0:T(8,128)(2,1)S(1)} %bitcast.150), custom_call_target="tpu_custom_call" | custom-call | flops 10737418240 | bytes 6291456 | tf_op jit(solution)/shard_map/pallas_call | solution.py:148
  162.6 1.3 fusion.77
  168.2 1.5 slice-done
  170.4 14.3 %shard_map.123 = bf16[384,1024]{1,0:T(8,128)(2,1)S(1)} custom-call(bf16[384,1024]{1,0:T(8,128)(2,1)S(1)} %pad_maximum_fusion.1.own_ref, bf16[1024,1024]{1,0:T(8,128)(2,1)S(1)} %bitcast.148, s32[2,512]{1,0:T(2,128)S(1)} %and_convert_fusion.usable_ref, bf16[8,4,3,128,256]{4,3,2,1,0:T(8,128)(2,1)S(1)} %bitcast.153), custom_call_target="tpu_custom_call" | custom-call | flops 10200547328 | bytes 6291456 | tf_op jit(solution)/shard_map/pallas_call | solution.py:148
  186.6 15.7 %all_gather.20 = bf16[4,80,768]{2,1,0:T(8,128)(2,1)S(1)} all-gather(bf16[1,80,768]{2,1,0:T(8,128)(2,1)S(1)} %pad_maximum_fusion.7), channel_id=1, replica_groups=mesh['dp'=8,'mp'=4] {'mp'}, dimensions={0}, use_global_device_ids=true | all-gather | bytes 614400 | tf_op jit(solution)/shard_map/all_gather | solution.py:307
  203.0 2.3 stack.98
  206.8 3.5 %all-to-all-start.2 = ((bf16[16,80,256]{2,1,0:T(8,128)(2,1)}), bf16[16,80,256]{2,1,0:T(8,128)(2,1)S(1)}, u32[]{:S(2)}, u32[]{:S(2)}) async-start(bf16[16,80,256]{2,1,0:T(8,128)(2,1)} %copy.109), calls=%async_computation.2 | async-start | bytes 1310720 | tf_op jit(solution)/shard_map/all_to_all | solution.py:316
  211.2 10.1 %all-to-all-done.2 = bf16[16,80,256]{2,1,0:T(8,128)(2,1)S(1)} async-done(((bf16[16,80,256]{2,1,0:T(8,128)(2,1)}), bf16[16,80,256]{2,1,0:T(8,128)(2,1)S(1)}, u32[]{:S(2)}, u32[]{:S(2)}) %all-to-all-start.2) | async-done | bytes 655392 | tf_op jit(solution)/shard_map/all_to_all | solution.py:316
  221.8 1.4 reshape.282
  223.2 2.2 reshape.293
  225.4 1.8 copy.114
  (159 shorter events, 24.2 us)
Async XLA Ops:
  7.2 1.7 copy-start
  7.2 65.6 %all-gather.7.cloned.1.call-start = ((), (), s32[]{:S(2)}) async-start(), calls=%async_computation.4 | async-start | bytes 2162688 | tf_op jit(solution)/shard_map/all_gather | solution.py:199
  8.8 134.9 %all-gather.5.cloned.1.call-start = ((), (), s32[]{:S(2)}) async-start(), calls=%async_computation.3 | async-start | bytes 6488064 | tf_op jit(solution)/shard_map/all_gather | solution.py:195
  22.1 0.7 copy-start.13
  22.7 7.3 %copy-start.11 = (s32[32]{0:T(128)S(1)}, s32[32]{0:T(128)}, u32[]{:S(2)}) copy-start(s32[32]{0:T(128)} %param.14) | copy-start | bytes 388
  22.7 7.3 %copy-start.12 = (s32[32]{0:T(128)S(1)}, s32[32]{0:T(128)}, u32[]{:S(2)}) copy-start(s32[32]{0:T(128)} %param.13) | copy-start | bytes 388
  24.4 30.1 %copy-start.5 = (bf16[160,1024]{1,0:T(8,128)(2,1)S(1)}, bf16[160,1024]{1,0:T(8,128)(2,1)}, u32[]{:S(2)}) copy-start(bf16[160,1024]{1,0:T(8,128)(2,1)} %param.16) | copy-start | bytes 983044
  24.4 15.7 %all-to-all-start = ((bf16[16,20,768]{2,1,0:T(8,128)(2,1)}), bf16[16,20,768]{2,1,0:T(8,128)(2,1)S(1)}, u32[]{:S(2)}, u32[]{:S(2)}) async-start(bf16[16,20,768]{2,1,0:T(8,128)(2,1)} %copy.96), calls=%async_computation | async-start | bytes 1179648 | tf_op jit(solution)/shard_map/all_to_all | solution.py:247
  41.1 12.9 %all-to-all-start.1 = ((bf16[8,20,768]{2,1,0:T(8,128)(2,1)}), bf16[8,20,768]{2,1,0:T(8,128)(2,1)S(1)}, u32[]{:S(2)}, u32[]{:S(2)}) async-start(bf16[8,20,768]{2,1,0:T(8,128)(2,1)} %copy.98), calls=%async_computation.1 | async-start | bytes 589824 | tf_op jit(solution)/shard_map/all_to_all | solution.py:258
  55.4 0.7 copy-start.10
  56.6 1.4 copy-start.1
  143.8 1.6 copy-start.2
  145.4 2.8 %copy-start.3 = (bf16[96,128,256]{2,1,0:T(8,128)(2,1)S(1)}, bf16[96,128,256]{2,1,0:T(8,128)(2,1)}, u32[]{:S(2)}) copy-start(bf16[96,128,256]{2,1,0:T(8,128)(2,1)} %all-gather.5.cloned.1.call-done) | copy-start | bytes 18874372
  148.1 14.4 %copy-start.4 = (bf16[4,8,32,1024]{3,2,1,0:T(8,128)(2,1)S(1)}, bf16[4,8,32,1024]{3,2,1,0:T(8,128)(2,1)}, u32[]{:S(2)}) copy-start(bf16[4,8,32,1024]{3,2,1,0:T(8,128)(2,1)} %copy.102) | copy-start | bytes 6291460
  148.2 14.4 %copy-start.6 = (f32[256,1024]{1,0:T(8,128)S(1)}, f32[256,1024]{1,0:T(8,128)}, u32[]{:S(2)}) copy-start(f32[256,1024]{1,0:T(8,128)} %get-tuple-element.8) | copy-start | bytes 3145732
  148.2 14.4 %copy-start.7 = (f32[256,1024]{1,0:T(8,128)S(1)}, f32[256,1024]{1,0:T(8,128)}, u32[]{:S(2)}) copy-start(f32[256,1024]{1,0:T(8,128)} %get-tuple-element.9) | copy-start | bytes 3145732
  163.9 0.9 copy-start.8
  164.0 0.9 copy-start.9
  167.5 2.2 slice-start
  167.7 2.8 %slice-start.1 = ((s8[6291456]{0:T(1024)(128)(4,1)}), s8[2097152]{0:T(1024)(128)(4,1)S(1)}, s32[]{:S(2)}) async-start(s8[6291456]{0:T(1024)(128)(4,1)} %bitcast.151), calls=%async_computation.6 | async-start | bytes 4194304
  206.8 14.6 %all-to-all-start.2 = ((bf16[16,80,256]{2,1,0:T(8,128)(2,1)}), bf16[16,80,256]{2,1,0:T(8,128)(2,1)S(1)}, u32[]{:S(2)}, u32[]{:S(2)}) async-start(bf16[16,80,256]{2,1,0:T(8,128)(2,1)} %copy.109), calls=%async_computation.2 | async-start | bytes 1310720 | tf_op jit(solution)/shard_map/all_to_all | solution.py:316
Sparse Core Ops, SparseCore 0:
  10.9 61.7 all-gather.6
  75.6 68.0 all-gather.4
where the time goes:
time: 235 us; the launch traced here: 234 us
  waiting for transfers between devices  105 us (45%)
  local copies, waits for them, and re-layouts  33.3 us (14%)
  Pallas kernels  28.7 us (12%)
  between operations  22.3 us (9%)
  blocking collectives  15.7 us (7%)
  starting transfers between devices  13.8 us (6%)
  other arithmetic  9.19 us (4%)
  matrix products  6.64 us (3%)
    all_gather x1, waiting for transfers between devices, gather_weights(): w_parts = lax.all_gather(part, ('dp', 'mp'), axis=0, tiled=False)  67.8 us
    pallas_call x2, Pallas kernels, attention(): pl.pallas_call(attention_kernel, grid=(groups,), out_shape=jax.ShapeDtype...  28.7 us
    all_gather x1, blocking collectives, shards(): both = lax.all_gather(both, 'mp')  15.7 us
    all_gather x1, waiting for transfers between devices, gather_weights(): out_parts = lax.all_gather(out_part, ('dp', 'mp'), axis=0, tiled=False)  13.1 us
    all_to_all x1, waiting for transfers between devices, shards(): lax.all_to_all(returned.astype(jnp.bfloat16), 'dp', split_axis=0, concat_...  10.1 us
    unnamed x36, local copies, waits for them, and re-layouts  8.54 us
    all_to_all x1, waiting for transfers between devices, shards(): mine = lax.all_to_all(spread, 'mp', split_axis=0, concat_axis=0, tiled=True)  8.03 us
    all_to_all x1, waiting for transfers between devices, shards(): lax.all_to_all(outgoing, 'dp', split_axis=0, concat_axis=0, tiled=True)  5.41 us
  transfers between devices with their start and end apart: 5, of which 5 were waited for; matrix products, arithmetic and copies ran while one was open for 9% of the time, Pallas kernels for 0%

commit v1 on v0

v1 whole, which is shorter than its diff:
```python
import functools
import math

import jax
import jax.numpy as jnp
import numpy as np
from jax import lax
from jax.experimental import pallas as pl
from jax.experimental.pallas import tpu as pltpu
from jax.sharding import PartitionSpec as P

MEL = 80
HEAD_DIM = 64
BLOCK = 256
CTX = 128
BLK_UTT = 4
UTT_DEV = 4
WORK_DEV = 6
EULER = 2
FRAMES = 2048
WIN = 512
SPAN_MAX = 1024
SLOT_DEV = 16
LANES = 128
PIECES = 8

flow_steps = 32.0
norm_eps = 1e-05
MESH = pl.DeviceIdType.MESH
VMEM_LIMIT = 60 * 1024 * 1024
F32 = jnp.float32
BF16 = jnp.bfloat16


def time_table(width):
    half = width // 2
    freqs = np.exp(-math.log(10000.0) * np.arange(half, dtype=np.float64) / half)
    rows = []
    for step in range(EULER):
        angles = 1000.0 * (step / flow_steps) * freqs
        rows.append(np.concatenate([np.sin(angles), np.cos(angles)]))
    return np.stack(rows).astype(np.float32)


def flip(index, bit):
    return index + bit * (1 - 2 * ((index // bit) % 2))


def pick(index, values):
    out = jnp.int32(values[-1])
    for i in range(len(values) - 1):
        out = jnp.where(index == i, jnp.int32(values[i]), out)
    return out


def shard_order(count):
    return [
        sorted((s for s in range(count) if s != m), key=lambda s: (abs(s - m), s))
        for m in range(count)
    ]


def remote(src, dst, send_sem, recv_sem, device):
    return pltpu.make_async_remote_copy(
        src_ref=src,
        dst_ref=dst,
        send_sem=send_sem,
        recv_sem=recv_sem,
        device_id=device,
        device_id_type=MESH,
    )


def enter(n_dp, n_mp, dp, mp):
    barrier = pltpu.get_barrier_semaphore()
    for t in range(1, n_dp):
        pl.semaphore_signal(
            barrier, inc=1, device_id={"dp": (dp + t) % n_dp}, device_id_type=MESH
        )
    for t in range(1, n_mp):
        pl.semaphore_signal(
            barrier, inc=1, device_id={"mp": (mp + t) % n_mp}, device_id_type=MESH
        )
    pl.semaphore_wait(barrier, n_dp + n_mp - 2)


def blocks_between(blocks_ref, worker, owner, capacity):
    blocks = [jnp.int32(-1)] * capacity
    slots = [jnp.int32(-1)] * capacity
    seen = jnp.int32(0)
    for j in range(WORK_DEV):
        block = blocks_ref[worker * WORK_DEV + j]
        mine = (block // SLOT_DEV) == owner
        for r in range(capacity):
            here = mine & (seen == r)
            blocks[r] = jnp.where(here, block, blocks[r])
            slots[r] = jnp.where(here, j, slots[r])
        seen = seen + mine.astype(jnp.int32)
    return blocks, slots


def choose(wanted, ids, parts):
    out = jnp.zeros_like(parts[0])
    for n, part in zip(ids, parts):
        out = jnp.where(wanted == n, part, out)
    return out


def pair_slots(mp):
    return 3 * (mp // 2) + 2 * (mp % 2), 3 * (mp // 2) + 1


class WeightGather:
    def __init__(self, n_mp, dp, mp, w_all, sems):
        self.n_mp, self.dp, self.mp, self.w_all = n_mp, dp, mp, w_all
        (self.zs, self.zf, self.zr, self.xs, self.xr, self.ys, self.yr, self.cs, self.cr) = sems
        self.rows = w_all.shape[2] // PIECES
        self.half = self.rows // 2
        base = dp - dp % PIECES
        part = dp % PIECES
        self.part = part
        self.x_peer = {"dp": base + flip(part, 2)}
        self.y_peer = {"dp": base + flip(part, 4)}
        self.c_peer = {"dp": base + flip(part, 1)}
        self.order = shard_order(n_mp)

    def view(self, shard, part, half):
        start = pl.multiple_of(part * self.rows + half * self.half, self.half)
        return self.w_all.at[shard, :, pl.ds(start, self.half), :]

    def shard(self, i):
        return pick(self.mp, [self.order[m][i] for m in range(self.n_mp)])

    def z_copy(self, shard, half, step, send_sem):
        view = self.view(shard, self.part, half)
        return remote(view, view, send_sem, self.zr.at[shard, half], {"mp": self.mp + step})

    def z_arrival(self, shard, half):
        view = self.view(shard, self.part, half)
        sem = self.zf.at[shard, half]
        return remote(view, view, sem, self.zr.at[shard, half], {"mp": (self.mp + 1) % self.n_mp})

    def send_own(self):
        @pl.when(self.mp + 1 < self.n_mp)
        def _():
            for half in range(2):
                self.z_copy(self.mp, half, 1, self.zs.at[0, half]).start()

        @pl.when(self.mp > 0)
        def _():
            for half in range(2):
                self.z_copy(self.mp, half, -1, self.zs.at[1, half]).start()

    def relay(self, shard, half, act):
        @pl.when((shard < self.mp) & (self.mp + 1 < self.n_mp))
        def _():
            act(self.z_copy(shard, half, 1, self.zf.at[shard, half]))

        @pl.when((shard > self.mp) & (self.mp > 0))
        def _():
            act(self.z_copy(shard, half, -1, self.zf.at[shard, half]))

    def x_copy(self, shard, part, half, kind):
        view = self.view(shard, part, half)
        return remote(
            view, view, self.xs.at[shard, kind], self.xr.at[shard, kind], self.x_peer
        )

    def y_copy(self, shard, part, half, kind):
        view = self.view(shard, part, half)
        return remote(
            view, view, self.ys.at[shard, kind], self.yr.at[shard, kind], self.y_peer
        )

    def c_copy(self, shard, part, half, kind):
        view = self.view(shard, part, half)
        return remote(
            view, view, self.cs.at[shard, kind], self.cr.at[shard, kind], self.c_peer
        )

    def own_piece(self, i):
        shard = self.shard(i)
        for half in range(2):
            self.z_arrival(shard, half).wait_recv()
            self.relay(shard, half, lambda copy: copy.start())
            self.x_copy(shard, self.part, half, half).start()
            self.y_copy(shard, self.part, half, half).start()
            self.c_copy(shard, self.part, half, half).start()

    def near_pieces(self, i):
        shard = self.shard(i)
        from_x, from_y = flip(self.part, 2), flip(self.part, 4)
        self.x_copy(shard, from_x, 0, 0).wait_recv()
        self.y_copy(shard, from_x, 0, 2).start()
        self.c_copy(shard, from_x, 0, 2).start()
        self.y_copy(shard, from_y, 0, 0).wait_recv()
        self.c_copy(shard, from_y, 0, 4).start()
        self.y_copy(shard, from_y, 1, 1).wait_recv()
        self.x_copy(shard, from_y, 1, 2).start()
        self.c_copy(shard, from_y, 1, 5).start()
        self.x_copy(shard, from_x, 1, 1).wait_recv()
        self.c_copy(shard, from_x, 1, 3).start()

    def far_pieces(self, i):
        shard = self.shard(i)
        far = flip(flip(self.part, 2), 4)
        self.y_copy(shard, far, 0, 2).wait_recv()
        self.c_copy(shard, far, 0, 6).start()
        self.x_copy(shard, far, 1, 2).wait_recv()
        self.c_copy(shard, far, 1, 7).start()

    def arrived(self, i):
        shard = self.shard(i)
        other = flip(self.part, 1)
        parts = [other, flip(other, 2), flip(other, 4), flip(flip(other, 2), 4)]
        for n, part in enumerate(parts):
            for half in range(2):
                self.c_copy(shard, part, half, 2 * n + half).wait_recv()

    def drain(self):
        for half in range(2):

            @pl.when(self.mp + 1 < self.n_mp)
            def _():
                self.z_copy(self.mp, half, 1, self.zs.at[0, half]).wait_send()

            @pl.when(self.mp > 0)
            def _():
                self.z_copy(self.mp, half, -1, self.zs.at[1, half]).wait_send()

        for i in range(self.n_mp - 1):
            shard = self.shard(i)
            for half in range(2):
                self.relay(shard, half, lambda copy: copy.wait_send())
            for kind in range(3):
                self.x_copy(shard, self.part, 0, kind).wait_send()
                self.y_copy(shard, self.part, 0, kind).wait_send()
            for kind in range(8):
                self.c_copy(shard, self.part, 0, kind).wait_send()


def gather_sems(n_mp):
    dma = pltpu.SemaphoreType.DMA
    return [
        dma((2, 2)),
        dma((n_mp, 2)),
        dma((n_mp, 2)),
        dma((n_mp, 3)),
        dma((n_mp, 3)),
        dma((n_mp, 3)),
        dma((n_mp, 3)),
        dma((n_mp, 8)),
        dma((n_mp, 8)),
    ]


def pack_windows(mel_ref, noise_ref, start_ref, length_ref, dp, mp, local):
    start = start_ref[dp * UTT_DEV + local]
    length = length_ref[dp * UTT_DEV + local]
    first = start - CTX + LANES * mp
    chunk = (first + LANES) // LANES
    offset = first + LANES - chunk * LANES
    count = 2 * BLK_UTT
    zero = jnp.zeros((MEL, LANES), BF16)
    chunks = [zero]
    for n in range(FRAMES // LANES):
        chunks.append(mel_ref[local, :, n * LANES : (n + 1) * LANES])
    bit = 1
    while 2 * bit <= len(chunks):
        bit *= 2
    while bit:
        moved = (chunk // bit) % 2 == 1
        keep = min(len(chunks), count + bit - 1)
        padded = chunks + [zero] * (keep + bit - len(chunks))
        chunks = [jnp.where(moved, padded[n + bit], padded[n]) for n in range(keep)]
        bit //= 2
    row = lax.broadcasted_iota(jnp.int32, (2 * LANES, LANES), 0)
    to = lax.broadcasted_iota(jnp.int32, (2 * LANES, LANES), 1)
    shift = jnp.where(row == to + offset, 1.0, 0.0).astype(BF16)
    both = jnp.concatenate(
        [jnp.concatenate(chunks[2 * k : 2 * k + 2], axis=1) for k in range(BLK_UTT)], axis=0
    )
    shifted = lax.dot_general(
        both, shift, (((1,), (0,)), ((), ())), preferred_element_type=F32
    )
    lane = lax.broadcasted_iota(jnp.int32, (MEL, LANES), 1)
    parts = []
    for k in range(BLK_UTT):
        frame = first + BLOCK * k + lane
        context = (frame >= 0) & (frame < FRAMES) & ((frame < start) | (frame >= start + length))
        own = jnp.minimum(BLOCK, length - BLOCK * k)
        place = LANES * (mp - 1) + lane
        state = (place >= 0) & (place < own)
        noise = jnp.where(
            mp == 2,
            noise_ref[local, :, BLOCK * k + LANES : BLOCK * k + 2 * LANES].astype(F32),
            noise_ref[local, :, BLOCK * k : BLOCK * k + LANES].astype(F32),
        )
        held = jnp.where(context, shifted[k * MEL : (k + 1) * MEL], 0.0)
        parts.append(jnp.where(state, noise, held).astype(BF16))
    return parts


def inbound_kernel(
    n_dp,
    n_mp,
    capacity,
    blocks_ref,
    start_ref,
    length_ref,
    mel_ref,
    noise_ref,
    w_qkv_ref,
    w_out_ref,
    w_all,
    win,
    packed,
    landed,
    sorted_parts,
    spread,
    load_sem,
    d_send,
    d_recv,
    m_send,
    m_recv,
    *w_sems,
):
    dp, mp = lax.axis_index("dp"), lax.axis_index("mp")
    width = w_all.shape[3]
    loads = [pltpu.make_async_copy(w_qkv_ref, w_all.at[mp, 0:3], load_sem.at[0])]
    for n in range(n_mp):
        loads.append(
            pltpu.make_async_copy(
                w_out_ref.at[:, n * width : (n + 1) * width],
                w_all.at[mp, 3, n * width : (n + 1) * width, :],
                load_sem.at[1 + n],
            )
        )
    for load in loads:
        load.start()
    enter(n_dp, n_mp, dp, mp)
    for load in loads:
        load.wait()
    gather = WeightGather(n_mp, dp, mp, w_all, w_sems)
    gather.send_own()

    def to_worker(t):
        worker = (dp + t) % n_dp
        return worker, remote(
            packed.at[worker], landed.at[dp], d_send.at[t], d_recv.at[t], {"dp": worker}
        )

    parts = []
    for local in range(UTT_DEV):
        parts += pack_windows(mel_ref, noise_ref, start_ref, length_ref, dp, mp, local)
    ids = [dp * SLOT_DEV + n for n in range(SLOT_DEV)]
    for t in range(1, n_dp + 1):
        worker, copy = to_worker(t)
        blocks, _ = blocks_between(blocks_ref, worker, dp, capacity)
        for r in range(capacity):
            part = choose(blocks[r], ids, parts)
            if t < n_dp:
                packed[worker, r] = part
            else:
                landed[dp, r] = part
        if t < n_dp:
            copy.start()
    for t in range(1, n_dp):
        to_worker(t)[1].wait_recv()

    ids, parts = [], []
    for owner in range(n_dp):
        blocks, _ = blocks_between(blocks_ref, dp, owner, capacity)
        ids += blocks
        parts += [landed[owner, r] for r in range(capacity)]
    for slot in range(WORK_DEV):
        sorted_parts[slot] = choose(blocks_ref[dp * WORK_DEV + slot], ids, parts)

    def to_place(t):
        place = (mp + t) % n_mp
        return place, remote(
            spread.at[place], win.at[mp], m_send.at[t], m_recv.at[t], {"mp": place}
        )

    for t in range(1, n_mp + 1):
        place, copy = to_place(t)
        for b, slot in enumerate(pair_slots(place)):
            if t < n_mp:
                spread[place, b] = sorted_parts[slot]
            else:
                win[mp, b] = sorted_parts[slot]
        if t < n_mp:
            copy.start()
    gather.own_piece(0)
    for t in range(1, n_mp):
        to_place(t)[1].wait_recv()
    gather.own_piece(1)
    gather.near_pieces(0)
    gather.far_pieces(0)
    gather.own_piece(2)
    gather.near_pieces(1)
    gather.far_pieces(1)
    gather.near_pieces(2)
    gather.far_pieces(2)
    for i in range(n_mp - 1):
        gather.arrived(i)
    for t in range(1, n_dp):
        to_worker(t)[1].wait_send()
    for t in range(1, n_mp):
        to_place(t)[1].wait_send()
    gather.drain()


def normalize(rows, gain):
    width = rows.shape[1]
    mean = jnp.sum(rows, axis=1, keepdims=True) * (1.0 / width)
    centred = rows - mean
    variance = jnp.sum(centred * centred, axis=1, keepdims=True) * (1.0 / width)
    return centred * lax.rsqrt(variance + norm_eps) * gain


def dot(a, b, contract):
    return lax.dot_general(a, b, ((contract[:1], contract[1:]), ((), ())), preferred_element_type=F32)


def steps_kernel(
    blocks_ref,
    start_ref,
    length_ref,
    win,
    w_input,
    attn_gain,
    w_all,
    final_gain,
    w_mel,
    embed,
    out_ref,
    state,
    residual,
    normed,
    keys,
    values_t,
    heads_t,
    heads,
):
    dp, mp = lax.axis_index("dp"), lax.axis_index("mp")
    groups, width, depth = w_all.shape[0], w_all.shape[3], w_all.shape[2]
    group_heads = width // HEAD_DIM
    half = BLOCK // 2
    tail = HEAD_DIM + 16
    first_row = (mp % 2) * half
    begins, counts = [], []
    for slot in pair_slots(mp):
        block = blocks_ref[dp * WORK_DEV + slot]
        order = block % BLK_UTT
        begins.append(start_ref[block // BLK_UTT] + BLOCK * order - CTX)
        counts.append(jnp.minimum(BLOCK, length_ref[block // BLK_UTT] - BLOCK * order))
    column = lax.broadcasted_iota(jnp.int32, (MEL, BLOCK), 1)
    live = [column < counts[b] for b in range(2)]
    for b in range(2):
        start = jnp.concatenate([win[1, b], win[2, b]], axis=1).astype(F32)
        state[b] = jnp.where(live[b], start, 0.0)
    lane = lax.broadcasted_iota(jnp.int32, (1, width), 1)
    for head in range(group_heads):
        ones = jnp.ones((16, 2 * WIN), BF16)
        values_t[head * tail + HEAD_DIM : (head + 1) * tail, :] = ones
    bias = []
    for b in range(2):
        frame = begins[b] + lax.broadcasted_iota(jnp.int32, (WIN, 1), 0)
        usable = (frame >= 0) & (frame < FRAMES)
        bias.append(jnp.where(usable, 0.0, -1e30).astype(F32))

    totals = None
    for step in range(EULER):
        last = step == EULER - 1
        sizes = (BLOCK, half if last else BLOCK)
        for b in range(2):
            for quarter in range(WIN // LANES):
                merged = win[quarter, b]
                inside = 0 < quarter < WIN // LANES - 1
                if inside:
                    at = slice((quarter - 1) * LANES, quarter * LANES)
                    held = jnp.where(live[b][:, at], 0.0, merged.astype(F32)).astype(BF16)
                    stacked = jnp.concatenate([held, state[b, :, at].astype(BF16)], axis=0)
                    hidden = dot(stacked.T, w_input[...], (1, 0))
                else:
                    hidden = dot(merged.T, w_input[0:MEL, :], (1, 0))
                hidden = hidden + embed[step : step + 1, :]
                row = b * WIN + quarter * LANES
                normed[row : row + LANES, :] = normalize(hidden, attn_gain[...]).astype(BF16)
                if inside:
                    row = b * BLOCK + (quarter - 1) * LANES
                    residual[row : row + LANES, :] = hidden

        def query_rows(b):
            offset = first_row if (last and b) else 0
            return offset, sizes[b]

        def group_body(g, carry):
            key_rows = dot(normed[...], w_all[g, 1], (1, 0)).astype(BF16)
            value_rows = dot(normed[...], w_all[g, 2], (1, 0)).astype(BF16)
            turned = value_rows.T
            for head in range(group_heads):
                values_t[head * tail : head * tail + HEAD_DIM, :] = turned[
                    head * HEAD_DIM : (head + 1) * HEAD_DIM
                ]
            for b in range(2):
                offset, count = query_rows(b)
                at = b * WIN + CTX + offset
                if not isinstance(at, int):
                    at = pl.multiple_of(at, LANES)
                rows = normed[pl.ds(at, count), :]
                scale = math.log2(math.e) / math.sqrt(HEAD_DIM)
                queries = (dot(rows, w_all[g, 0], (1, 0)) * scale).astype(BF16)
                block_keys = key_rows[b * WIN : (b + 1) * WIN].astype(F32)
                edge = [
                    jnp.where(lane == width - 1, bias[b], block_keys).astype(BF16),
                    jnp.where(lane == 0, bias[b], block_keys).astype(BF16),
                ]
                for head in range(group_heads):
                    upper = head >= group_heads // 2
                    flag_lane = 0 if upper else width - 1
                    mine = (lane // HEAD_DIM) == head
                    flag = jnp.where(lane == flag_lane, 1.0, 0.0).astype(BF16)
                    masked = jnp.where(mine, queries, flag)
                    scores = dot(edge[int(upper)], masked, (1, 1))
                    top = jnp.max(scores, axis=0, keepdims=True)
                    weights = jnp.exp2(scores - top).astype(BF16)
                    product = dot(
                        values_t[head * tail : (head + 1) * tail, b * WIN : (b + 1) * WIN],
                        weights,
                        (1, 0),
                    )
                    norm = product[HEAD_DIM : HEAD_DIM + 1, :]
                    out = product[:HEAD_DIM] * (1.0 / norm)
                    heads_t[
                        head * HEAD_DIM : (head + 1) * HEAD_DIM, b * BLOCK : b * BLOCK + count
                    ] = out.astype(BF16)
            lanes = pl.ds(pl.multiple_of(g * width, width), width)
            used = BLOCK + sizes[1]
            heads[0:used, lanes] = heads_t[:, 0:used].T
            return carry

        lax.fori_loop(0, groups, group_body, 0)

        velocities = []
        for b in range(2):
            offset, count = query_rows(b)
            at = b * BLOCK + offset
            if not isinstance(at, int):
                at = pl.multiple_of(at, LANES)
            columns = []
            for n in range(depth // width):
                lanes = slice(n * width, (n + 1) * width)
                term = residual[pl.ds(at, count), lanes]
                for g in range(groups):
                    term = term + dot(
                        heads[b * BLOCK : b * BLOCK + count, g * width : (g + 1) * width],
                        w_all[g, 3, n * width : (n + 1) * width, :],
                        (1, 0),
                    )
                columns.append(term)
            final = normalize(jnp.concatenate(columns, axis=1), final_gain[...]).astype(BF16)
            velocities.append(dot(w_mel[...], final, (1, 1)))
        if not last:
            velocities = [jnp.where(live[b], velocities[b], 0.0) for b in range(2)]
            for b in range(2):
                state[b] = state[b] + velocities[b] * (1.0 / flow_steps)
            second = jnp.where(mp % 2 == 0, velocities[1][:, :half], velocities[1][:, half:])
            part = [velocities[0], second]
            totals = part if totals is None else [totals[b] + part[b] for b in range(2)]
        else:
            places = column[:, :half] + first_row
            part = [
                jnp.where(live[0], velocities[0], 0.0),
                jnp.where(places < counts[1], velocities[1], 0.0),
            ]
            totals = [totals[b] + part[b] for b in range(2)]
            out_ref[0, :, 0:BLOCK] = totals[0].astype(BF16)
            out_ref[0, :, BLOCK : BLOCK + half] = totals[1].astype(BF16)
            out_ref[1, :, 0:BLOCK] = part[0].astype(BF16)
            out_ref[1, :, BLOCK : BLOCK + half] = part[1].astype(BF16)


def outbound_kernel(
    n_dp,
    n_mp,
    capacity,
    blocks_ref,
    mine_ref,
    filled_ref,
    velocity_ref,
    column,
    packed,
    landed,
    m_send,
    m_recv,
    d_send,
    d_recv,
):
    dp, mp = lax.axis_index("dp"), lax.axis_index("mp")
    half = BLOCK // 2
    enter(n_dp, n_mp, dp, mp)

    def to_place(t):
        return remote(
            mine_ref, column.at[mp], m_send.at[t], m_recv.at[t], {"mp": (mp + t) % n_mp}
        )

    for t in range(1, n_mp):
        to_place(t).start()
    column[mp] = mine_ref[...]
    for t in range(1, n_mp):
        to_place(t).wait_recv()

    def block_of(kind, slot):
        pair, which = slot // 3, slot % 3
        one, other = 2 * pair, 2 * pair + 1
        if which == 0:
            return column[one, kind, :, 0:BLOCK]
        if which == 2:
            return column[other, kind, :, 0:BLOCK]
        return jnp.concatenate(
            [column[m, kind, :, BLOCK : BLOCK + half] for m in (one, other)], axis=1
        )

    parts = [block_of(0, slot) for slot in range(WORK_DEV)]

    def to_owner(t):
        owner = (dp + t) % n_dp
        return owner, remote(
            packed.at[owner], landed.at[dp], d_send.at[t], d_recv.at[t], {"dp": owner}
        )

    for t in range(1, n_dp + 1):
        owner, copy = to_owner(t)
        _, places = blocks_between(blocks_ref, dp, owner, capacity)
        for r in range(capacity):
            part = choose(places[r], range(WORK_DEV), parts)
            if t < n_dp:
                packed[owner, r] = part
            else:
                landed[dp, r] = part
        if t < n_dp:
            copy.start()
    for slot in range(WORK_DEV):
        velocity_ref[slot] = block_of(1, slot).astype(F32)
    for t in range(1, n_dp):
        to_owner(t)[1].wait_recv()
    ids, parts = [], []
    for worker in range(n_dp):
        blocks, _ = blocks_between(blocks_ref, worker, dp, capacity)
        ids += blocks
        parts += [landed[worker, r] for r in range(capacity)]
    for local in range(SLOT_DEV):
        order = local % BLK_UTT
        filled_ref[local // BLK_UTT, :, order * BLOCK : (order + 1) * BLOCK] = choose(
            dp * SLOT_DEV + local, ids, parts
        ).astype(F32)
    for t in range(1, n_mp):
        to_place(t).wait_send()
    for t in range(1, n_dp):
        to_owner(t)[1].wait_send()


def shards(
    n_dp,
    n_mp,
    mel_audio,
    start_noise,
    span_start,
    span_length,
    block_route,
    w_input,
    attn_gain,
    w_qkv,
    w_out,
    final_gain,
    w_mel,
):
    capacity = (SLOT_DEV + n_dp - 1) // n_dp
    depth, width = w_qkv.shape[0], w_qkv.shape[2]
    slot_ids = jnp.arange(n_dp * WORK_DEV, dtype=jnp.int32)
    every_slot = jnp.arange(block_route.shape[0], dtype=jnp.int32)
    matches = block_route[None, :] == slot_ids[:, None]
    blocks = jnp.sum(jnp.where(matches, every_slot[None, :], 0), axis=1)

    smem = pl.BlockSpec(memory_space=pltpu.SMEM)
    vmem = pl.BlockSpec(memory_space=pltpu.VMEM)
    hbm = pl.BlockSpec(memory_space=pl.ANY)
    dma = pltpu.SemaphoreType.DMA
    quarters = WIN // LANES
    w_all, win = pl.pallas_call(
        functools.partial(inbound_kernel, n_dp, n_mp, capacity),
        out_shape=(
            jax.ShapeDtypeStruct((n_mp, 4, depth, width), BF16),
            jax.ShapeDtypeStruct((quarters, 2, MEL, LANES), BF16),
        ),
        in_specs=[smem, smem, smem, vmem, vmem, hbm, hbm],
        out_specs=(vmem, vmem),
        scratch_shapes=[
            pltpu.VMEM((n_dp, capacity, MEL, LANES), BF16),
            pltpu.VMEM((n_dp, capacity, MEL, LANES), BF16),
            pltpu.VMEM((WORK_DEV, MEL, LANES), BF16),
            pltpu.VMEM((n_mp, 2, MEL, LANES), BF16),
            dma((1 + n_mp,)),
            dma((n_dp,)),
            dma((n_dp,)),
            dma((n_mp,)),
            dma((n_mp,)),
            *gather_sems(n_mp),
        ],
        compiler_params=pltpu.CompilerParams(
            collective_id=0, has_side_effects=True, vmem_limit_bytes=VMEM_LIMIT
        ),
        name="inbound",
    )(
        blocks,
        span_start,
        span_length,
        mel_audio,
        start_noise,
        w_qkv.transpose(1, 0, 2),
        w_out,
    )

    group_heads = width // HEAD_DIM
    tail = HEAD_DIM + 16
    mine = pl.pallas_call(
        steps_kernel,
        out_shape=jax.ShapeDtypeStruct((2, MEL, BLOCK + BLOCK // 2), BF16),
        in_specs=[smem, smem, smem, vmem, vmem, vmem, vmem, vmem, vmem, vmem],
        out_specs=vmem,
        scratch_shapes=[
            pltpu.VMEM((2, MEL, BLOCK), F32),
            pltpu.VMEM((2 * BLOCK, depth), F32),
            pltpu.VMEM((2 * WIN, depth), BF16),
            pltpu.VMEM((2 * WIN, width), BF16),
            pltpu.VMEM((group_heads * tail, 2 * WIN), BF16),
            pltpu.VMEM((width, 2 * BLOCK), BF16),
            pltpu.VMEM((2 * BLOCK, depth), BF16),
        ],
        compiler_params=pltpu.CompilerParams(vmem_limit_bytes=VMEM_LIMIT),
        name="steps",
    )(
        blocks,
        span_start,
        span_length,
        win,
        w_input,
        attn_gain.reshape(1, -1),
        w_all,
        final_gain.reshape(1, -1),
        w_mel,
        jnp.asarray(time_table(depth)),
    )

    return pl.pallas_call(
        functools.partial(outbound_kernel, n_dp, n_mp, capacity),
        out_shape=(
            jax.ShapeDtypeStruct((UTT_DEV, MEL, SPAN_MAX), F32),
            jax.ShapeDtypeStruct((WORK_DEV, MEL, BLOCK), F32),
        ),
        in_specs=[smem, vmem],
        out_specs=(vmem, vmem),
        scratch_shapes=[
            pltpu.VMEM((n_mp, 2, MEL, BLOCK + BLOCK // 2), BF16),
            pltpu.VMEM((n_dp, capacity, MEL, BLOCK), BF16),
            pltpu.VMEM((n_dp, capacity, MEL, BLOCK), BF16),
            dma((n_mp,)),
            dma((n_mp,)),
            dma((n_dp,)),
            dma((n_dp,)),
        ],
        compiler_params=pltpu.CompilerParams(
            collective_id=1, has_side_effects=True, vmem_limit_bytes=VMEM_LIMIT
        ),
        name="outbound",
    )(blocks, mine)


def solution(mesh):
    n_dp, n_mp = mesh.shape["dp"], mesh.shape["mp"]
    return jax.shard_map(
        functools.partial(shards, n_dp, n_mp),
        mesh=mesh,
        in_specs=(
            P("dp", None, None),
            P("dp", None, None),
            P(),
            P(),
            P(),
            P(),
            P(),
            P(None, None, "mp"),
            P("mp", None),
            P(),
            P(),
        ),
        out_specs=(P("dp", None, None), P("dp", None, None)),
        check_vma=False,
    )
```

time: 235 us -> 135 us (0.57)
  waiting for transfers between devices: 105 us -> 0 us
  Pallas kernels: 28.7 us -> 128 us
  local copies, waits for them, and re-layouts: 33.3 us -> 3.36 us
  between operations: 22.3 us -> 0.66 us
  blocking collectives: 15.7 us -> 0 us
  starting transfers between devices: 13.8 us -> 0 us
  other arithmetic: 9.19 us -> 1.28 us
  matrix products: 6.64 us -> 0 us
    pallas_call x2 -> x3, Pallas kernels: 28.7 us -> 128 us  [the longest x1 54.2 us: shards(): pl.pallas_call(functools.partial(inbound_kernel, n_dp, n_mp, capacity), o...]
    all_gather x2 -> x0, waiting for transfers between devices: 80.9 us -> none  [the longest x1 67.8 us: gather_weights(): w_parts = lax.all_gather(part, ('dp', 'mp'), axis=0, tiled=False)]
    all_to_all x3 -> x0, waiting for transfers between devices: 23.6 us -> none  [the longest x1 10.1 us: shards(): lax.all_to_all(returned.astype(jnp.bfloat16), 'dp', split_axis=0, concat_...]
    all_gather x1 -> x0, blocking collectives: 15.7 us -> none  [shards(): both = lax.all_gather(both, 'mp')]
    all_to_all x3 -> x0, starting transfers between devices: 13.7 us -> none  [the longest x1 5.33 us: shards(): lax.all_to_all(outgoing, 'dp', split_axis=0, concat_axis=0, tiled=True)]
    dot_general x10 -> x0, matrix products: 6.64 us -> none  [the longest x2 2.4 us: block_velocity(): attended = jnp.dot(head_outputs, w_out, preferred_element_type=jnp.float32)]
    reshape x5 -> x0, local copies, waits for them, and re-layouts: 5.75 us -> none  [the longest x2 4 us: to_span(): return slot_values.reshape(UTT_DEV, BLK_UTT, MEL, BLOCK).transpose(0, 2,...]
    unnamed x36 -> x4, local copies, waits for them, and re-layouts: 8.54 us -> 3.36 us
  transfers between devices with their start and end apart: 5 -> 0, of which waited for: 5 -> 0; matrix products, arithmetic and copies ran while one was open for 9% -> 0% of each run, Pallas kernels for 0% -> 0%
where the time goes in v1:
time: 135 us; the launch traced here: 134 us
  Pallas kernels  128 us (95%)
  local copies, waits for them, and re-layouts  3.36 us (2%)
    pallas_call x1, Pallas kernels, shards(): pl.pallas_call(functools.partial(inbound_kernel, n_dp, n_mp, capacity), o...  54.2 us
    pallas_call x1, Pallas kernels, shards(): pl.pallas_call(steps_kernel, out_shape=jax.ShapeDtypeStruct((2, MEL, BLOC...  52.1 us
    pallas_call x1, Pallas kernels, shards(): pl.pallas_call(functools.partial(outbound_kernel, n_dp, n_mp, capacity),...  22.2 us
    unnamed x4, local copies, waits for them, and re-layouts  3.36 us

profile of v1, /device:TPU:0, one launch (start us, length us, event | category | flops | bytes accessed | tf_op | source)
XLA Modules:
  0.0 133.8 jit_solution(9202070100540440637)
XLA Ops:
  0.6 1.3 select_reduce_fusion.blocks_ref
  1.9 54.2 %inbound.1 = (bf16[4,4,1024,256]{3,2,1,0:T(8,128)(2,1)}, bf16[4,2,80,128]{3,2,1,0:T(8,128)(2,1)}) custom-call(s32[48]{0:T(128)} %select_reduce_fusion.blocks_ref, s32[32]{0:T(128)} %start_ref.3, s32[32]{0:T(128)} %length_ref.3, bf16[4,80,2048]{2,1,0:T(8,128)(2,1)} %mel_ref.1, bf16[4,80,1024]{2,1,0:T(8,128)(2,1)} %noise_ref.1, bf16[3,1024,256]{2,1,0:T(8,128)(2,1)} %bitcast.3, ...), custom_call_target="tpu_custom_call" | custom-call | tf_op jit(solution)/shard_map/inbound/pallas_call | solution.py:693
  56.1 52.1 %steps.1.mine_ref = bf16[2,80,384]{2,1,0:T(8,128)(2,1)} custom-call(s32[48]{0:T(128)} %select_reduce_fusion.blocks_ref, s32[32]{0:T(128)} %start_ref.3, s32[32]{0:T(128)} %length_ref.3, bf16[4,2,80,128]{3,2,1,0:T(8,128)(2,1)} %get-tuple-element.4.win, bf16[160,1024]{1,0:T(8,128)(2,1)} %w_input.1, f32[1,1024]{1,0:T(1,128)} %bitcast.4, ...), custom_call_target="tpu_custom_call" | custom-call | tf_op jit(solution)/shard_map/steps/pallas_call | solution.py:729
  108.2 22.2 %outbound.1 = (f32[4,80,1024]{2,1,0:T(8,128)}, f32[6,80,256]{2,1,0:T(8,128)}) custom-call(s32[48]{0:T(128)} %select_reduce_fusion.blocks_ref, bf16[2,80,384]{2,1,0:T(8,128)(2,1)} %steps.1.mine_ref), custom_call_target="tpu_custom_call" | custom-call | tf_op jit(solution)/shard_map/outbound/pallas_call | solution.py:758
  130.4 0.0 copy-start
  130.4 2.6 %copy.16 = f32[4,80,1024]{2,1,0:T(8,128)} copy(f32[4,80,1024]{2,1,0:T(8,128)} %get-tuple-element.8) | data formatting | bytes 2621440
  133.0 0.0 copy-done
  133.0 0.8 copy.17
Async XLA Ops:
  130.4 2.6 %copy-start = (f32[6,80,256]{2,1,0:T(8,128)S(1)}, f32[6,80,256]{2,1,0:T(8,128)}, u32[]{:S(2)}) copy-start(f32[6,80,256]{2,1,0:T(8,128)} %get-tuple-element.9) | copy-start | bytes 1474564

commit v2 on v1

--- a/solution.py
+++ b/solution.py
@@ -89,7 +89,7 @@
     slots = [jnp.int32(-1)] * capacity
     seen = jnp.int32(0)
     for j in range(WORK_DEV):
-        block = blocks_ref[worker * WORK_DEV + j]
+        block = blocks_ref[0, worker * WORK_DEV + j]
         mine = (block // SLOT_DEV) == owner
         for r in range(capacity):
             here = mine & (seen == r)
@@ -301,32 +301,184 @@
     return parts
 
 
-def inbound_kernel(
+def normalize(rows, gain):
+    width = rows.shape[1]
+    mean = jnp.sum(rows, axis=1, keepdims=True) * (1.0 / width)
+    centred = rows - mean
+    variance = jnp.sum(centred * centred, axis=1, keepdims=True) * (1.0 / width)
+    return centred * lax.rsqrt(variance + norm_eps) * gain
+
+
+def dot(a, b, contract):
+    return lax.dot_general(a, b, ((contract[:1], contract[1:]), ((), ())), preferred_element_type=F32)
+
+
+class Steps:
+    def __init__(self, plan_ref, dp, mp, win, w_all, weights, scratch):
+        self.mp, self.win, self.w_all = mp, win, w_all
+        self.w_input, self.attn_gain, self.final_gain, self.w_mel, self.embed = weights
+        self.state, self.residual, self.normed, self.values_t, self.heads_t, self.heads = scratch
+        self.groups, self.depth, self.width = w_all.shape[0], w_all.shape[2], w_all.shape[3]
+        self.group_heads = self.width // HEAD_DIM
+        self.half = BLOCK // 2
+        self.first_row = (mp % 2) * self.half
+        begins, counts = [], []
+        for slot in pair_slots(mp):
+            at = dp * WORK_DEV + slot
+            order = plan_ref[0, at] % BLK_UTT
+            begins.append(plan_ref[1, at] + BLOCK * order - CTX)
+            counts.append(jnp.minimum(BLOCK, plan_ref[2, at] - BLOCK * order))
+        self.counts = counts
+        column = lax.broadcasted_iota(jnp.int32, (MEL, BLOCK), 1)
+        self.column = column
+        self.live = [column < counts[b] for b in range(2)]
+        self.lane = lax.broadcasted_iota(jnp.int32, (1, self.width), 1)
+        self.bias = []
+        for b in range(2):
+            frame = begins[b] + lax.broadcasted_iota(jnp.int32, (WIN, 1), 0)
+            usable = (frame >= 0) & (frame < FRAMES)
+            self.bias.append(jnp.where(usable, 0.0, -1e30).astype(F32))
+
+    def begin(self):
+        for b in range(2):
+            start = jnp.concatenate([self.win[1, b], self.win[2, b]], axis=1).astype(F32)
+            self.state[b] = jnp.where(self.live[b], start, 0.0)
+        self.values_t[self.width : self.width + 16, :] = jnp.ones((16, 2 * WIN), BF16)
+
+    def hidden(self, step, b):
+        for quarter in range(WIN // LANES):
+            merged = self.win[quarter, b]
+            inside = 0 < quarter < WIN // LANES - 1
+            if inside:
+                at = slice((quarter - 1) * LANES, quarter * LANES)
+                held = jnp.where(self.live[b][:, at], 0.0, merged.astype(F32)).astype(BF16)
+                stacked = jnp.concatenate([held, self.state[b, :, at].astype(BF16)], axis=0)
+                hidden = dot(stacked.T, self.w_input[...], (1, 0))
+            else:
+                hidden = dot(merged.T, self.w_input[0:MEL, :], (1, 0))
+            hidden = hidden + self.embed[step : step + 1, :]
+            row = b * WIN + quarter * LANES
+            self.normed[row : row + LANES, :] = normalize(hidden, self.attn_gain[...]).astype(BF16)
+            if inside:
+                row = b * BLOCK + (quarter - 1) * LANES
+                self.residual[row : row + LANES, :] = hidden
+
+    def rows_of(self, last, b):
+        if last and b:
+            return self.first_row, self.half
+        return 0, BLOCK
+
+    def project(self, g):
+        keys = dot(self.normed[...], self.w_all[g, 1], (1, 0)).astype(BF16)
+        values = dot(self.normed[...], self.w_all[g, 2], (1, 0)).astype(BF16)
+        self.values_t[0 : self.width, :] = values.T
+        return keys
+
+    def attend(self, last, g, b, keys):
+        offset, count = self.rows_of(last, b)
+        at = b * WIN + CTX + offset
+        if not isinstance(at, int):
+            at = pl.multiple_of(at, LANES)
+        scale = math.log2(math.e) / math.sqrt(HEAD_DIM)
+        queries = (dot(self.normed[pl.ds(at, count), :], self.w_all[g, 0], (1, 0)) * scale).astype(BF16)
+        block_keys = keys[b * WIN : (b + 1) * WIN].astype(F32)
+        weights = []
+        for upper in range(2):
+            flag_lane = 0 if upper else self.width - 1
+            flagged = jnp.where(self.lane == flag_lane, self.bias[b], block_keys).astype(BF16)
+            flag = jnp.where(self.lane == flag_lane, 1.0, 0.0).astype(BF16)
+            masked = []
+            for head in range(self.group_heads // 2):
+                mine = (self.lane // HEAD_DIM) == head + upper * (self.group_heads // 2)
+                masked.append(jnp.where(mine, queries, flag))
+            scores = dot(flagged, jnp.concatenate(masked, axis=0), (1, 1))
+            top = jnp.max(scores, axis=0, keepdims=True)
+            weights.append(jnp.exp2(scores - top).astype(BF16))
+        weights = jnp.concatenate(weights, axis=1)
+        at = slice(b * WIN, (b + 1) * WIN)
+        for head in range(self.group_heads):
+            rows = slice(head * HEAD_DIM, (head + 1) * HEAD_DIM)
+            with_ones = jnp.concatenate(
+                [self.values_t[rows, at], self.values_t[self.width : self.width + 16, at]], axis=0
+            )
+            product = dot(with_ones, weights[:, head * count : (head + 1) * count], (1, 0))
+            out = product[:HEAD_DIM] * (1.0 / product[HEAD_DIM : HEAD_DIM + 1])
+            self.heads_t[rows, b * BLOCK : b * BLOCK + count] = out.astype(BF16)
+
+    def collect(self, last, g):
+        lanes = pl.ds(pl.multiple_of(g * self.width, self.width), self.width)
+        used = BLOCK + self.rows_of(last, 1)[1]
+        self.heads[0:used, lanes] = self.heads_t[:, 0:used].T
+
+    def velocity(self, last, b):
+        offset, count = self.rows_of(last, b)
+        at = b * BLOCK + offset
+        if not isinstance(at, int):
+            at = pl.multiple_of(at, LANES)
+        columns = []
+        for n in range(self.depth // self.width):
+            lanes = slice(n * self.width, (n + 1) * self.width)
+            term = self.residual[pl.ds(at, count), lanes]
+            for g in range(self.groups):
+                term = term + dot(
+                    self.heads[b * BLOCK : b * BLOCK + count, g * self.width : (g + 1) * self.width],
+                    self.w_all[g, 3, lanes, :],
+                    (1, 0),
+                )
+            columns.append(term)
+        final = normalize(jnp.concatenate(columns, axis=1), self.final_gain[...]).astype(BF16)
+        result = dot(self.w_mel[...], final, (1, 1))
+        return jnp.where(self.column[:, :count] + offset < self.counts[b], result, 0.0)
+
+
+def whole_kernel(
     n_dp,
     n_mp,
     capacity,
-    blocks_ref,
+    plan_ref,
     start_ref,
     length_ref,
     mel_ref,
     noise_ref,
     w_qkv_ref,
     w_out_ref,
+    w_input,
+    attn_gain,
+    final_gain,
+    w_mel,
+    embed,
+    filled_ref,
+    velocity_ref,
     w_all,
     win,
     packed,
     landed,
     sorted_parts,
     spread,
+    state,
+    residual,
+    normed,
+    values_t,
+    heads_t,
+    heads,
+    mine_ref,
+    column,
+    packed_out,
+    landed_out,
     load_sem,
     d_send,
     d_recv,
     m_send,
     m_recv,
+    mo_send,
+    mo_recv,
+    do_send,
+    do_recv,
     *w_sems,
 ):
     dp, mp = lax.axis_index("dp"), lax.axis_index("mp")
     width = w_all.shape[3]
+    half = BLOCK // 2
     loads = [pltpu.make_async_copy(w_qkv_ref, w_all.at[mp, 0:3], load_sem.at[0])]
     for n in range(n_mp):
         loads.append(
@@ -343,6 +495,7 @@
         load.wait()
     gather = WeightGather(n_mp, dp, mp, w_all, w_sems)
     gather.send_own()
+    blocks_ref = plan_ref
 
     def to_worker(t):
         worker = (dp + t) % n_dp
@@ -365,6 +518,7 @@
                 landed[dp, r] = part
         if t < n_dp:
             copy.start()
+    gather.own_piece(0)
     for t in range(1, n_dp):
         to_worker(t)[1].wait_recv()
 
@@ -374,7 +528,7 @@
         ids += blocks
         parts += [landed[owner, r] for r in range(capacity)]
     for slot in range(WORK_DEV):
-        sorted_parts[slot] = choose(blocks_ref[dp * WORK_DEV + slot], ids, parts)
+        sorted_parts[slot] = choose(blocks_ref[0, dp * WORK_DEV + slot], ids, parts)
 
     def to_place(t):
         place = (mp + t) % n_mp
@@ -391,227 +545,75 @@
                 win[mp, b] = sorted_parts[slot]
         if t < n_mp:
             copy.start()
-    gather.own_piece(0)
+    gather.near_pieces(0)
     for t in range(1, n_mp):
         to_place(t)[1].wait_recv()
+    steps = Steps(
+        plan_ref,
+        dp,
+        mp,
+        win,
+        w_all,
+        (w_input, attn_gain, final_gain, w_mel, embed),
+        (state, residual, normed, values_t, heads_t, heads),
+    )
+    steps.begin()
     gather.own_piece(1)
-    gather.near_pieces(0)
+    steps.hidden(0, 0)
     gather.far_pieces(0)
-    gather.own_piece(2)
+    steps.hidden(0, 1)
     gather.near_pieces(1)
-    gather.far_pieces(1)
-    gather.near_pieces(2)
-    gather.far_pieces(2)
-    for i in range(n_mp - 1):
-        gather.arrived(i)
-    for t in range(1, n_dp):
-        to_worker(t)[1].wait_send()
+    calls = [
+        [lambda: gather.own_piece(2), lambda: gather.far_pieces(1), lambda: gather.arrived(0)],
+        [lambda: gather.near_pieces(2), lambda: gather.far_pieces(2), lambda: gather.arrived(1)],
+        [lambda: None, lambda: None, lambda: gather.arrived(2)],
+        [lambda: None, lambda: None, lambda: None],
+    ]
+    for n in range(n_mp):
+        g = gather.shard(n - 1) if n else mp
+        keys = steps.project(g)
+        calls[n][0]()
+        steps.attend(False, g, 0, keys)
+        calls[n][1]()
+        steps.attend(False, g, 1, keys)
+        steps.collect(False, g)
+        calls[n][2]()
+    totals = []
+    for b in range(2):
+        moved = steps.velocity(False, b)
+        state[b] = state[b] + moved * (1.0 / flow_steps)
+        if b:
+            moved = jnp.where(mp % 2 == 0, moved[:, :half], moved[:, half:])
+        totals.append(moved)
+
+    for step in range(1, EULER):
+        for b in range(2):
+            steps.hidden(step, b)
+
+        def group_body(g, carry):
+            keys = steps.project(g)
+            for b in range(2):
+                steps.attend(True, g, b, keys)
+            steps.collect(True, g)
+            return carry
+
+        lax.fori_loop(0, n_mp, group_body, 0)
+    for b in range(2):
+        moved = steps.velocity(True, b)
+        at = slice(0, BLOCK) if b == 0 else slice(BLOCK, BLOCK + half)
+        mine_ref[0, :, at] = (totals[b] + moved).astype(BF16)
+        mine_ref[1, :, at] = moved.astype(BF16)
+
+    def to_column(t):
+        return remote(
+            mine_ref, column.at[mp], mo_send.at[t], mo_recv.at[t], {"mp": (mp + t) % n_mp}
+        )
+
     for t in range(1, n_mp):
-        to_place(t)[1].wait_send()
-    gather.drain()
-
-
-def normalize(rows, gain):
-    width = rows.shape[1]
-    mean = jnp.sum(rows, axis=1, keepdims=True) * (1.0 / width)
-    centred = rows - mean
-    variance = jnp.sum(centred * centred, axis=1, keepdims=True) * (1.0 / width)
-    return centred * lax.rsqrt(variance + norm_eps) * gain
-
-
-def dot(a, b, contract):
-    return lax.dot_general(a, b, ((contract[:1], contract[1:]), ((), ())), preferred_element_type=F32)
-
-
-def steps_kernel(
-    blocks_ref,
-    start_ref,
-    length_ref,
-    win,
-    w_input,
-    attn_gain,
-    w_all,
-    final_gain,
-    w_mel,
-    embed,
-    out_ref,
-    state,
-    residual,
-    normed,
-    keys,
-    values_t,
-    heads_t,
-    heads,
-):
-    dp, mp = lax.axis_index("dp"), lax.axis_index("mp")
-    groups, width, depth = w_all.shape[0], w_all.shape[3], w_all.shape[2]
-    group_heads = width // HEAD_DIM
-    half = BLOCK // 2
-    tail = HEAD_DIM + 16
-    first_row = (mp % 2) * half
-    begins, counts = [], []
-    for slot in pair_slots(mp):
-        block = blocks_ref[dp * WORK_DEV + slot]
-        order = block % BLK_UTT
-        begins.append(start_ref[block // BLK_UTT] + BLOCK * order - CTX)
-        counts.append(jnp.minimum(BLOCK, length_ref[block // BLK_UTT] - BLOCK * order))
-    column = lax.broadcasted_iota(jnp.int32, (MEL, BLOCK), 1)
-    live = [column < counts[b] for b in range(2)]
-    for b in range(2):
-        start = jnp.concatenate([win[1, b], win[2, b]], axis=1).astype(F32)
-        state[b] = jnp.where(live[b], start, 0.0)
-    lane = lax.broadcasted_iota(jnp.int32, (1, width), 1)
-    for head in range(group_heads):
-        ones = jnp.ones((16, 2 * WIN), BF16)
-        values_t[head * tail + HEAD_DIM : (head + 1) * tail, :] = ones
-    bias = []
-    for b in range(2):
-        frame = begins[b] + lax.broadcasted_iota(jnp.int32, (WIN, 1), 0)
-        usable = (frame >= 0) & (frame < FRAMES)
-        bias.append(jnp.where(usable, 0.0, -1e30).astype(F32))
-
-    totals = None
-    for step in range(EULER):
-        last = step == EULER - 1
-        sizes = (BLOCK, half if last else BLOCK)
-        for b in range(2):
-            for quarter in range(WIN // LANES):
-                merged = win[quarter, b]
-                inside = 0 < quarter < WIN // LANES - 1
-                if inside:
-                    at = slice((quarter - 1) * LANES, quarter * LANES)
-                    held = jnp.where(live[b][:, at], 0.0, merged.astype(F32)).astype(BF16)
-                    stacked = jnp.concatenate([held, state[b, :, at].astype(BF16)], axis=0)
-                    hidden = dot(stacked.T, w_input[...], (1, 0))
-                else:
-                    hidden = dot(merged.T, w_input[0:MEL, :], (1, 0))
-                hidden = hidden + embed[step : step + 1, :]
-                row = b * WIN + quarter * LANES
-                normed[row : row + LANES, :] = normalize(hidden, attn_gain[...]).astype(BF16)
-                if inside:
-                    row = b * BLOCK + (quarter - 1) * LANES
-                    residual[row : row + LANES, :] = hidden
-
-        def query_rows(b):
-            offset = first_row if (last and b) else 0
-            return offset, sizes[b]
-
-        def group_body(g, carry):
-            key_rows = dot(normed[...], w_all[g, 1], (1, 0)).astype(BF16)
-            value_rows = dot(normed[...], w_all[g, 2], (1, 0)).astype(BF16)
-            turned = value_rows.T
-            for head in range(group_heads):
-                values_t[head * tail : head * tail + HEAD_DIM, :] = turned[
-                    head * HEAD_DIM : (head + 1) * HEAD_DIM
-                ]
-            for b in range(2):
-                offset, count = query_rows(b)
-                at = b * WIN + CTX + offset
-                if not isinstance(at, int):
-                    at = pl.multiple_of(at, LANES)
-                rows = normed[pl.ds(at, count), :]
-                scale = math.log2(math.e) / math.sqrt(HEAD_DIM)
-                queries = (dot(rows, w_all[g, 0], (1, 0)) * scale).astype(BF16)
-                block_keys = key_rows[b * WIN : (b + 1) * WIN].astype(F32)
-                edge = [
-                    jnp.where(lane == width - 1, bias[b], block_keys).astype(BF16),
-                    jnp.where(lane == 0, bias[b], block_keys).astype(BF16),
-                ]
-                for head in range(group_heads):
-                    upper = head >= group_heads // 2
-                    flag_lane = 0 if upper else width - 1
-                    mine = (lane // HEAD_DIM) == head
-                    flag = jnp.where(lane == flag_lane, 1.0, 0.0).astype(BF16)
-                    masked = jnp.where(mine, queries, flag)
-                    scores = dot(edge[int(upper)], masked, (1, 1))
-                    top = jnp.max(scores, axis=0, keepdims=True)
-                    weights = jnp.exp2(scores - top).astype(BF16)
-                    product = dot(
-                        values_t[head * tail : (head + 1) * tail, b * WIN : (b + 1) * WIN],
-                        weights,
-                        (1, 0),
-                    )
-                    norm = product[HEAD_DIM : HEAD_DIM + 1, :]
-                    out = product[:HEAD_DIM] * (1.0 / norm)
-                    heads_t[
-                        head * HEAD_DIM : (head + 1) * HEAD_DIM, b * BLOCK : b * BLOCK + count
-                    ] = out.astype(BF16)
-            lanes = pl.ds(pl.multiple_of(g * width, width), width)
-            used = BLOCK + sizes[1]
-            heads[0:used, lanes] = heads_t[:, 0:used].T
-            return carry
-
-        lax.fori_loop(0, groups, group_body, 0)
-
-        velocities = []
-        for b in range(2):
-            offset, count = query_rows(b)
-            at = b * BLOCK + offset
-            if not isinstance(at, int):
-                at = pl.multiple_of(at, LANES)
-            columns = []
-            for n in range(depth // width):
-                lanes = slice(n * width, (n + 1) * width)
-                term = residual[pl.ds(at, count), lanes]
-                for g in range(groups):
-                    term = term + dot(
-                        heads[b * BLOCK : b * BLOCK + count, g * width : (g + 1) * width],
-                        w_all[g, 3, n * width : (n + 1) * width, :],
-                        (1, 0),
-                    )
-                columns.append(term)
-            final = normalize(jnp.concatenate(columns, axis=1), final_gain[...]).astype(BF16)
-            velocities.append(dot(w_mel[...], final, (1, 1)))
-        if not last:
-            velocities = [jnp.where(live[b], velocities[b], 0.0) for b in range(2)]
-            for b in range(2):
-                state[b] = state[b] + velocities[b] * (1.0 / flow_steps)
-            second = jnp.where(mp % 2 == 0, velocities[1][:, :half], velocities[1][:, half:])
-            part = [velocities[0], second]
-            totals = part if totals is None else [totals[b] + part[b] for b in range(2)]
-        else:
-            places = column[:, :half] + first_row
-            part = [
-                jnp.where(live[0], velocities[0], 0.0),
-                jnp.where(places < counts[1], velocities[1], 0.0),
-            ]
-            totals = [totals[b] + part[b] for b in range(2)]
-            out_ref[0, :, 0:BLOCK] = totals[0].astype(BF16)
-            out_ref[0, :, BLOCK : BLOCK + half] = totals[1].astype(BF16)
-            out_ref[1, :, 0:BLOCK] = part[0].astype(BF16)
-            out_ref[1, :, BLOCK : BLOCK + half] = part[1].astype(BF16)
-
-
-def outbound_kernel(
-    n_dp,
-    n_mp,
-    capacity,
-    blocks_ref,
-    mine_ref,
-    filled_ref,
-    velocity_ref,
-    column,
-    packed,
-    landed,
-    m_send,
-    m_recv,
-    d_send,
-    d_recv,
-):
-    dp, mp = lax.axis_index("dp"), lax.axis_index("mp")
-    half = BLOCK // 2
-    enter(n_dp, n_mp, dp, mp)
-
-    def to_place(t):
-        return remote(
-            mine_ref, column.at[mp], m_send.at[t], m_recv.at[t], {"mp": (mp + t) % n_mp}
-        )
-
-    for t in range(1, n_mp):
-        to_place(t).start()
+        to_column(t).start()
     column[mp] = mine_ref[...]
     for t in range(1, n_mp):
-        to_place(t).wait_recv()
+        to_column(t).wait_recv()
 
     def block_of(kind, slot):
         pair, which = slot // 3, slot % 3
@@ -626,41 +628,46 @@
 
     parts = [block_of(0, slot) for slot in range(WORK_DEV)]
 
-    def to_owner(t):
+    def to_home(t):
         owner = (dp + t) % n_dp
         return owner, remote(
-            packed.at[owner], landed.at[dp], d_send.at[t], d_recv.at[t], {"dp": owner}
+            packed_out.at[owner], landed_out.at[dp], do_send.at[t], do_recv.at[t], {"dp": owner}
         )
 
     for t in range(1, n_dp + 1):
-        owner, copy = to_owner(t)
+        owner, copy = to_home(t)
         _, places = blocks_between(blocks_ref, dp, owner, capacity)
         for r in range(capacity):
             part = choose(places[r], range(WORK_DEV), parts)
             if t < n_dp:
-                packed[owner, r] = part
+                packed_out[owner, r] = part
             else:
-                landed[dp, r] = part
+                landed_out[dp, r] = part
         if t < n_dp:
             copy.start()
     for slot in range(WORK_DEV):
-        velocity_ref[slot] = block_of(1, slot).astype(F32)
+        velocity_ref[slot] = block_of(1, slot)
     for t in range(1, n_dp):
-        to_owner(t)[1].wait_recv()
+        to_home(t)[1].wait_recv()
     ids, parts = [], []
     for worker in range(n_dp):
         blocks, _ = blocks_between(blocks_ref, worker, dp, capacity)
         ids += blocks
-        parts += [landed[worker, r] for r in range(capacity)]
+        parts += [landed_out[worker, r] for r in range(capacity)]
     for local in range(SLOT_DEV):
         order = local % BLK_UTT
         filled_ref[local // BLK_UTT, :, order * BLOCK : (order + 1) * BLOCK] = choose(
             dp * SLOT_DEV + local, ids, parts
-        ).astype(F32)
+        )
     for t in range(1, n_mp):
-        to_place(t).wait_send()
+        to_column(t).wait_send()
     for t in range(1, n_dp):
-        to_owner(t)[1].wait_send()
+        to_home(t)[1].wait_send()
+    for t in range(1, n_dp):
+        to_worker(t)[1].wait_send()
+    for t in range(1, n_mp):
+        to_place(t)[1].wait_send()
+    gather.drain()
 
 
 def shards(
@@ -683,100 +690,71 @@
     slot_ids = jnp.arange(n_dp * WORK_DEV, dtype=jnp.int32)
     every_slot = jnp.arange(block_route.shape[0], dtype=jnp.int32)
     matches = block_route[None, :] == slot_ids[:, None]
-    blocks = jnp.sum(jnp.where(matches, every_slot[None, :], 0), axis=1)
+    facts = jnp.stack(
+        [every_slot, jnp.repeat(span_start, BLK_UTT), jnp.repeat(span_length, BLK_UTT)]
+    )
+    plan = jnp.sum(jnp.where(matches[None], facts[:, None, :], 0), axis=2)
 
     smem = pl.BlockSpec(memory_space=pltpu.SMEM)
     vmem = pl.BlockSpec(memory_space=pltpu.VMEM)
     hbm = pl.BlockSpec(memory_space=pl.ANY)
     dma = pltpu.SemaphoreType.DMA
     quarters = WIN // LANES
-    w_all, win = pl.pallas_call(
-        functools.partial(inbound_kernel, n_dp, n_mp, capacity),
+    filled, velocity = pl.pallas_call(
+        functools.partial(whole_kernel, n_dp, n_mp, capacity),
         out_shape=(
-            jax.ShapeDtypeStruct((n_mp, 4, depth, width), BF16),
-            jax.ShapeDtypeStruct((quarters, 2, MEL, LANES), BF16),
+            jax.ShapeDtypeStruct((UTT_DEV, MEL, SPAN_MAX), BF16),
+            jax.ShapeDtypeStruct((WORK_DEV, MEL, BLOCK), BF16),
         ),
-        in_specs=[smem, smem, smem, vmem, vmem, hbm, hbm],
+        in_specs=[smem, smem, smem, vmem, vmem, hbm, hbm, vmem, vmem, vmem, vmem, vmem],
         out_specs=(vmem, vmem),
         scratch_shapes=[
+            pltpu.VMEM((n_mp, 4, depth, width), BF16),
+            pltpu.VMEM((quarters, 2, MEL, LANES), BF16),
             pltpu.VMEM((n_dp, capacity, MEL, LANES), BF16),
             pltpu.VMEM((n_dp, capacity, MEL, LANES), BF16),
             pltpu.VMEM((WORK_DEV, MEL, LANES), BF16),
             pltpu.VMEM((n_mp, 2, MEL, LANES), BF16),
+            pltpu.VMEM((2, MEL, BLOCK), F32),
+            pltpu.VMEM((2 * BLOCK, depth), F32),
+            pltpu.VMEM((2 * WIN, depth), BF16),
+            pltpu.VMEM((width + 16, 2 * WIN), BF16),
+            pltpu.VMEM((width, 2 * BLOCK), BF16),
+            pltpu.VMEM((2 * BLOCK, depth), BF16),
+            pltpu.VMEM((2, MEL, BLOCK + BLOCK // 2), BF16),
+            pltpu.VMEM((n_mp, 2, MEL, BLOCK + BLOCK // 2), BF16),
+            pltpu.VMEM((n_dp, capacity, MEL, BLOCK), BF16),
+            pltpu.VMEM((n_dp, capacity, MEL, BLOCK), BF16),
             dma((1 + n_mp,)),
             dma((n_dp,)),
             dma((n_dp,)),
             dma((n_mp,)),
             dma((n_mp,)),
+            dma((n_mp,)),
+            dma((n_mp,)),
+            dma((n_dp,)),
+            dma((n_dp,)),
             *gather_sems(n_mp),
         ],
         compiler_params=pltpu.CompilerParams(
             collective_id=0, has_side_effects=True, vmem_limit_bytes=VMEM_LIMIT
         ),
-        name="inbound",
+        name="whole",
     )(
-        blocks,
+        plan,
         span_start,
         span_length,
         mel_audio,
         start_noise,
         w_qkv.transpose(1, 0, 2),
         w_out,
-    )
-
-    group_heads = width // HEAD_DIM
-    tail = HEAD_DIM + 16
-    mine = pl.pallas_call(
-        steps_kernel,
-        out_shape=jax.ShapeDtypeStruct((2, MEL, BLOCK + BLOCK // 2), BF16),
-        in_specs=[smem, smem, smem, vmem, vmem, vmem, vmem, vmem, vmem, vmem],
-        out_specs=vmem,
-        scratch_shapes=[
-            pltpu.VMEM((2, MEL, BLOCK), F32),
-            pltpu.VMEM((2 * BLOCK, depth), F32),
-            pltpu.VMEM((2 * WIN, depth), BF16),
-            pltpu.VMEM((2 * WIN, width), BF16),
-            pltpu.VMEM((group_heads * tail, 2 * WIN), BF16),
-            pltpu.VMEM((width, 2 * BLOCK), BF16),
-            pltpu.VMEM((2 * BLOCK, depth), BF16),
-        ],
-        compiler_params=pltpu.CompilerParams(vmem_limit_bytes=VMEM_LIMIT),
-        name="steps",
-    )(
-        blocks,
-        span_start,
-        span_length,
-        win,
         w_input,
         attn_gain.reshape(1, -1),
-        w_all,
         final_gain.reshape(1, -1),
         w_mel,
         jnp.asarray(time_table(depth)),
     )
-
-    return pl.pallas_call(
-        functools.partial(outbound_kernel, n_dp, n_mp, capacity),
-        out_shape=(
-            jax.ShapeDtypeStruct((UTT_DEV, MEL, SPAN_MAX), F32),
-            jax.ShapeDtypeStruct((WORK_DEV, MEL, BLOCK), F32),
-        ),
-        in_specs=[smem, vmem],
-        out_specs=(vmem, vmem),
-        scratch_shapes=[
-            pltpu.VMEM((n_mp, 2, MEL, BLOCK + BLOCK // 2), BF16),
-            pltpu.VMEM((n_dp, capacity, MEL, BLOCK), BF16),
-            pltpu.VMEM((n_dp, capacity, MEL, BLOCK), BF16),
-            dma((n_mp,)),
-            dma((n_mp,)),
-            dma((n_dp,)),
-            dma((n_dp,)),
-        ],
-        compiler_params=pltpu.CompilerParams(
-            collective_id=1, has_side_effects=True, vmem_limit_bytes=VMEM_LIMIT
-        ),
-        name="outbound",
-    )(blocks, mine)
+    return filled.astype(F32), velocity.astype(F32)
 
 
 def solution(mesh):

time: 135 us -> 95 us (0.70)
  Pallas kernels: 128 us -> 87.4 us
  other arithmetic: 1.28 us -> 4.55 us
  local copies, waits for them, and re-layouts: 3.36 us -> 1.67 us
    pallas_call x3 -> x1, Pallas kernels: 128 us -> 87.4 us  [shards(): pl.pallas_call(functools.partial(whole_kernel, n_dp, n_mp, capacity), out...]
    unnamed x4 -> x2, local copies, waits for them, and re-layouts: 3.36 us -> 0.01 us
    convert_element_type x0 -> x2, other arithmetic: none -> 3.15 us  [shards(): return (filled.astype(F32), velocity.astype(F32))]
    broadcast_in_dim x0 -> x2, local copies, waits for them, and re-layouts: none -> 1.46 us  [the longest x1 0.73 us: shards(): jnp.repeat(span_length, BLK_UTT)]
where the time goes in v2:
time: 95 us; the launch traced here: 94.3 us
  Pallas kernels  87.4 us (92%)
  other arithmetic  4.55 us (5%)
  local copies, waits for them, and re-layouts  1.67 us (2%)
    pallas_call x1, Pallas kernels, shards(): pl.pallas_call(functools.partial(whole_kernel, n_dp, n_mp, capacity), out...  87.4 us
    convert_element_type x2, other arithmetic, shards(): return (filled.astype(F32), velocity.astype(F32))  3.15 us

profile of v2, /device:TPU:0, one launch (start us, length us, event | category | flops | bytes accessed | tf_op | source)
XLA Modules:
  0.0 94.3 jit_solution(4422874231423109657)
XLA Ops:
  0.6 0.7 broadcast_in_dim.31
  1.4 0.1 stack_reshape.6
  1.5 0.7 broadcast_in_dim.32
  2.2 0.1 stack_reshape.7
  2.3 0.7 iota_compare_fusion
  3.0 0.7 select_reduce_fusion.plan_ref
  3.7 87.4 %whole.1 = (bf16[4,80,1024]{2,1,0:T(8,128)(2,1)}, bf16[6,80,256]{2,1,0:T(8,128)(2,1)}) custom-call(s32[3,48]{1,0:T(4,128)} %select_reduce_fusion.plan_ref, s32[32]{0:T(128)} %start_ref.1, s32[32]{0:T(128)} %length_ref.1, bf16[4,80,2048]{2,1,0:T(8,128)(2,1)} %mel_ref.1, bf16[4,80,1024]{2,1,0:T(8,128)(2,1)} %noise_ref.1, bf16[3,1024,256]{2,1,0:T(8,128)(2,1)} %bitcast.3, ...), custom_call_target="tpu_custom_call" | custom-call | tf_op jit(solution)/shard_map/whole/pallas_call | solution.py:703
  91.1 0.0 copy-start
  91.1 2.3 %convert_element_type.6 = f32[4,80,1024]{2,1,0:T(8,128)} convert(bf16[4,80,1024]{2,1,0:T(8,128)(2,1)} %get-tuple-element.4) | non-fusion elementwise | flops 327680 | bytes 1966080 | tf_op jit(solution)/shard_map/convert_element_type | solution.py:757
  93.5 0.0 copy-done
  93.5 0.8 convert_element_type.7
  (2 shorter events, 0.0 us)
Async XLA Ops:
  91.1 2.3 %copy-start = (bf16[6,80,256]{2,1,0:T(8,128)(2,1)S(1)}, bf16[6,80,256]{2,1,0:T(8,128)(2,1)}, u32[]{:S(2)}) copy-start(bf16[6,80,256]{2,1,0:T(8,128)(2,1)} %get-tuple-element.5) | copy-start | bytes 737284
